TPU v7x, 256 devices: a whole 4x4x8 slice. The times are simulated.
256 devices in a mesh: row: 16 (over x, y), col: 16 (over z, core).
Axes of the slice: x: 4, y: 4, z: 8, core: 2. Of those that a mesh axis runs over, the one named last changes fastest.
Arguments:
- inputs: bfloat16 [2048, 16384], P('col', 'row'), may hold values from -6 to 6
- weight: bfloat16 [16384, 16384], P('row', 'col'), may hold values from -0.046875 to 0.046875
- cotangent: bfloat16 [2048, 16384], P('row', 'col'), may hold values from -0.75 to 0.75
- scale_in: float32 [8, 16384], P(None, 'row'), may hold values from -4 to 4
- scale_out: float32 [8, 16384], P(None, 'col'), may hold values from -4 to 4
- member: int32 [2048], replicated, may hold values from 0 to 7
Outputs:
- input_grad: bfloat16 [2048, 16384], P('col', 'row')
- weight_grad: float32 [16384, 16384], P('row', 'col')
- in_factor_grad: float32 [8, 16384], P(None, 'row')
- out_factor_grad: float32 [8, 16384], P(None, 'col')
All inputs are finite; a program needn't handle non-finite values.
Results may differ from a plain program's by a relative error of at most 0.0049.
Values may be sent and summed in bfloat16 or wider, within the bound.
No kernel may reach another device: no remote copies, remote signals or barrier semaphores. Data moves between devices by JAX's collectives and lax.ppermute only.
A program may use at most 128 MiB of HBM per device.

v0:
```python
import jax
import jax.numpy as jnp
from jax import lax
from jax.sharding import PartitionSpec as P

highest = lax.Precision.HIGHEST


def from_everyone(value, axis):
    copies = jnp.broadcast_to(value, (lax.axis_size(axis), *value.shape))
    return lax.all_to_all(copies, axis, split_axis=0, concat_axis=0, tiled=True)


def of_everyone(value, axis):
    return from_everyone(value, axis).sum(axis=0)


def gathered_total(value, axis):
    return lax.all_gather(value, axis).sum(0)


def member_sums(one_hot, values):
    return jnp.dot(one_hot.T, values, precision=highest)


def local(inputs, weight, cotangent, scale_in, scale_out, member):
    n_members = scale_in.shape[0]
    one_hot = (member[:, None] == jnp.arange(n_members, dtype=jnp.int32)[None, :]).astype(
        jnp.float32
    )
    full_inputs = lax.all_gather(inputs, "col", axis=0, tiled=True)
    full_cot = lax.all_gather(cotangent, "row", axis=0, tiled=True)
    r_rows = jnp.dot(one_hot, scale_in, precision=highest)
    s_rows = jnp.dot(one_hot, scale_out, precision=highest)
    scaled_in = (full_inputs * r_rows).astype(jnp.bfloat16)
    scaled_cot = (full_cot * s_rows).astype(jnp.bfloat16)
    batch = scaled_in.shape[0]
    pre_part = jnp.dot(scaled_in, weight, preferred_element_type=jnp.float32)
    out_term = member_sums(one_hot, full_cot.astype(jnp.float32) * pre_part)
    out_factor_grad = of_everyone(out_term, "row")
    col_share = batch // lax.axis_size("col")
    col_start = lax.axis_index("col") * col_share
    back_part = lax.dot_general(
        scaled_cot, weight, (((1,), (1,)), ((), ())), preferred_element_type=jnp.float32
    )
    in_term = member_sums(one_hot, full_inputs.astype(jnp.float32) * back_part)
    in_factor_grad = gathered_total(in_term, "col")
    back_block = lax.psum_scatter(back_part, "col", scatter_dimension=0, tiled=True)
    r_block = lax.dynamic_slice_in_dim(r_rows, col_start, col_share, 0)
    input_grad = (back_block * r_block).astype(jnp.bfloat16)
    weight_grad = lax.dot_general(
        scaled_in, scaled_cot, (((0,), (0,)), ((), ())), preferred_element_type=jnp.float32
    )
    return (input_grad, weight_grad, in_factor_grad, out_factor_grad)


def solution(mesh):
    placed = (
        P("col", "row"),
        P("row", "col"),
        P("row", "col"),
        P(None, "row"),
        P(None, "col"),
        P(),
    )
    return jax.shard_map(
        local,
        mesh=mesh,
        in_specs=placed,
        out_specs=(P("col", "row"), P("row", "col"), P(None, "row"), P(None, "col")),
        check_vma=False,
    )
```

profile of v0, /device:TPU:2, one launch (start us, length us, event | category | flops | bytes accessed | tf_op | source)
XLA Modules:
  0.0 195.8 jit_solution(3907940686163401925)
XLA Ops:
  7.2 0.0 copy-start
  7.2 0.0 all-gather.4.cloned.1.call-start
  7.2 0.7 all-gather.4.cloned.1.call-update
  7.9 0.0 all-gather.6.cloned.1.call-start
  8.0 0.7 all-gather.6.cloned.1.call-update
  8.7 0.0 reduce-scatter.2.cloned.1.call-start
  8.7 61.1 %all-gather.4.cloned.1.call-done = bf16[2048,1024]{1,0:T(8,128)(2,1)} async-done(((bf16[128,1024]{1,0:T(8,128)(2,1)}), bf16[2048,1024]{1,0:T(8,128)(2,1)}) %all-gather.4.cloned.1.call-update) | async-done | bytes 4194320 | tf_op jit(solution)/shard_map/all_gather | solution.py:32
  69.8 5.6 %fusion = bf16[2048,1024]{1,0:T(8,128)(2,1)S(1)} fusion(bf16[2048,1024]{1,0:T(8,128)(2,1)} %all-gather.4.cloned.1.call-done, f32[8,1024]{1,0:T(8,128)} %param.10, s32[2048]{0:T(1024)} %param.11), kind=kOutput, calls=%fused_computation.4 | convolution fusion | flops 207634432 | bytes 8429568 | tf_op jit(solution)/shard_map/dot_general | solution.py:34
  75.4 0.0 copy-start.2
  75.4 2.0 copy-done.2
  77.4 0.0 copy-done
  77.4 7.1 %fusion.13 = f32[2048,1024]{1,0:T(8,128)} fusion(bf16[2048,1024]{1,0:T(8,128)(2,1)S(1)} %fusion, bf16[1024,1024]{1,0:T(8,128)(2,1)S(1)} %copy-done), kind=kOutput, calls=%fused_computation.18 | convolution fusion | flops 4294967296 | bytes 14680064 | tf_op jit(solution)/shard_map/dot_general | solution.py:43
  84.4 0.0 copy-start.4
  84.4 0.0 copy-start.5
  84.4 0.0 reduce-scatter.2.cloned.1.call-update
  84.5 0.7 copy-done.4
  85.1 0.1 copy-done.5
  85.2 5.6 %fusion.4 = f32[2048,1024]{1,0:T(8,128)} fusion(f32[8,1024]{1,0:T(8,128)S(1)} %copy-done.5, s32[2048]{0:T(1024)S(1)} %copy-done.4), kind=kOutput, calls=%fused_computation.9 | convolution fusion | flops 201342976 | bytes 8429568 | tf_op jit(solution)/shard_map/dot_general | solution.py:33
  90.8 22.5 %all-gather.6.cloned.1.call-done = bf16[2048,1024]{1,0:T(8,128)(2,1)} async-done(((bf16[128,1024]{1,0:T(8,128)(2,1)}), bf16[2048,1024]{1,0:T(8,128)(2,1)}) %all-gather.6.cloned.1.call-update) | async-done | bytes 4194320 | tf_op jit(solution)/shard_map/all_gather | solution.py:31
  113.3 0.0 copy-start.1
  113.3 7.7 %fusion.9 = f32[2048,1024]{1,0:T(8,128)S(1)} fusion(bf16[1024,1024]{1,0:T(8,128)(2,1)S(1)} %copy-done, f32[2048,1024]{1,0:T(8,128)} %fusion.4, bf16[2048,1024]{1,0:T(8,128)(2,1)} %all-gather.6.cloned.1.call-done), kind=kOutput, calls=%fused_computation.16 | convolution fusion | flops 4301258752 | bytes 23068672 | tf_op jit(solution)/shard_map/dot_general | solution.py:38
  121.0 0.0 copy-done.1
  121.0 3.4 %fusion.1 = f32[8,1024]{1,0:T(8,128)S(1)} fusion(f32[2048,1024]{1,0:T(8,128)S(1)} %fusion.9, bf16[2048,1024]{1,0:T(8,128)(2,1)S(1)} %copy-done.1, s32[2048]{0:T(1024)S(1)} %copy-done.4), kind=kOutput, calls=%fused_computation.5 | convolution fusion | flops 205537280 | bytes 12623872 | tf_op jit(solution)/shard_map/dot_general | solution.py:23
  124.5 0.9 broadcast_in_dim.2
  125.3 7.3 %all-to-all-start = ((f32[16,8,1024]{2,1,0:T(8,128)}), f32[16,8,1024]{2,1,0:T(8,128)S(1)}, u32[]{:S(2)}, u32[]{:S(2)}) async-start(f32[16,8,1024]{2,1,0:T(8,128)} %broadcast_in_dim.2), calls=%async_computation.1 | async-start | bytes 1048576 | tf_op jit(solution)/shard_map/all_to_all | solution.py:11
  132.6 0.0 copy-start.3
  132.6 12.9 %fusion.11 = f32[1024,1024]{1,0:T(8,128)} fusion(bf16[2048,1024]{1,0:T(8,128)(2,1)} %copy-done.2, f32[2048,1024]{1,0:T(8,128)} %fusion.4, bf16[2048,1024]{1,0:T(8,128)(2,1)} %all-gather.6.cloned.1.call-done), kind=kOutput, calls=%fused_computation.17 | convolution fusion | flops 4301258752 | bytes 20971520 | tf_op jit(solution)/shard_map/dot_general | solution.py:51
  145.5 0.0 copy-done.3
  145.5 5.9 %fusion.3 = f32[8,1024]{1,0:T(8,128)S(1)} fusion(f32[2048,1024]{1,0:T(8,128)} %fusion.13, bf16[2048,1024]{1,0:T(8,128)(2,1)S(1)} %copy-done.3, s32[2048]{0:T(1024)S(1)} %copy-done.4), kind=kOutput, calls=%fused_computation.7 | convolution fusion | flops 205537280 | bytes 12623872 | tf_op jit(solution)/shard_map/dot_general | solution.py:23
  151.4 18.8 %all-gather = f32[128,1024]{1,0:T(8,128)S(1)} all-gather(f32[8,1024]{1,0:T(8,128)S(1)} %fusion.3), channel_id=2, replica_groups=mesh['row'=16,'col'=16] {'col'}, dimensions={0}, use_global_device_ids=true | all-gather | bytes 557056 | tf_op jit(solution)/shard_map/all_gather | solution.py:19
  170.2 0.6 bitcast_reduce_fusion
  170.9 0.0 all-to-all-done
  170.9 0.6 reduce_sum.19
  171.5 15.8 %reduce-scatter.2.cloned.1.call-done = f32[128,1024]{1,0:T(8,128)} async-done(((f32[2048,1024]{1,0:T(8,128)}), f32[128,1024]{1,0:T(8,128)}) %reduce-scatter.2.cloned.1.call-update) | async-done | bytes 524304 | tf_op jit(solution)/shard_map/reduce_scatter | solution.py:48
  187.4 2.0 %multiply_convert_fusion = bf16[128,1024]{1,0:T(8,128)(2,1)} fusion(f32[128,1024]{1,0:T(8,128)} %reduce-scatter.2.cloned.1.call-done, f32[2048,1024]{1,0:T(8,128)} %fusion.4, s32[]{:T(128)S(6)} %select_n.3), kind=kLoop, calls=%fused_computation.11 | loop fusion | flops 262144 | bytes 1310724 | tf_op jit(solution)/shard_map/convert_element_type | solution.py:50
Async XLA Ops:
  7.2 70.2 %copy-start = (bf16[1024,1024]{1,0:T(8,128)(2,1)S(1)}, bf16[1024,1024]{1,0:T(8,128)(2,1)}, u32[]{:S(2)}) copy-start(bf16[1024,1024]{1,0:T(8,128)(2,1)} %param.7) | copy-start | bytes 6291460
  7.2 62.6 %all-gather.4.cloned.1.call-start = ((), (), s32[]{:S(2)}) async-start(), calls=%async_computation.2 | async-start | bytes 4456448 | tf_op jit(solution)/shard_map/all_gather | solution.py:32
  7.9 105.4 %all-gather.6.cloned.1.call-start = ((), (), s32[]{:S(2)}) async-start(), calls=%async_computation.4 | async-start | bytes 4456448 | tf_op jit(solution)/shard_map/all_gather | solution.py:31
  8.7 178.7 %reduce-scatter.2.cloned.1.call-start = ((), (), s32[]{:S(2)}) async-start(), calls=%async_computation.3 | async-start | bytes 8912896 | tf_op jit(solution)/shard_map/reduce_scatter | solution.py:48
  75.4 2.0 %copy-start.2 = (bf16[2048,1024]{1,0:T(8,128)(2,1)}, bf16[2048,1024]{1,0:T(8,128)(2,1)S(1)}, u32[]{:S(2)}) copy-start(bf16[2048,1024]{1,0:T(8,128)(2,1)S(1)} %fusion) | copy-start | bytes 12582916
  84.4 0.7 copy-start.4
  84.4 0.8 copy-start.5
  113.3 7.7 %copy-start.1 = (bf16[2048,1024]{1,0:T(8,128)(2,1)S(1)}, bf16[2048,1024]{1,0:T(8,128)(2,1)}, u32[]{:S(2)}) copy-start(bf16[2048,1024]{1,0:T(8,128)(2,1)} %all-gather.4.cloned.1.call-done) | copy-start | bytes 12582916
  125.3 45.5 %all-to-all-start = ((f32[16,8,1024]{2,1,0:T(8,128)}), f32[16,8,1024]{2,1,0:T(8,128)S(1)}, u32[]{:S(2)}, u32[]{:S(2)}) async-start(f32[16,8,1024]{2,1,0:T(8,128)} %broadcast_in_dim.2), calls=%async_computation.1 | async-start | bytes 1048576 | tf_op jit(solution)/shard_map/all_to_all | solution.py:11
  132.6 12.9 %copy-start.3 = (bf16[2048,1024]{1,0:T(8,128)(2,1)S(1)}, bf16[2048,1024]{1,0:T(8,128)(2,1)}, u32[]{:S(2)}) copy-start(bf16[2048,1024]{1,0:T(8,128)(2,1)} %all-gather.6.cloned.1.call-done) | copy-start | bytes 12582916
Sparse Core Ops, SparseCore 0:
  10.4 59.3 all-gather.3
  71.7 41.6 all-gather.5
  115.9 71.4 reduce-scatter.1
where the time goes:
time: 196 us
  waiting for transfers between devices  101 us (52%)
  matrix products  48.2 us (25%)
  blocking collectives  18.8 us (10%)
  between operations  13.8 us (7%)
  starting transfers between devices  7.39 us (4%)
  local copies, waits for them, and re-layouts  3.59 us (2%)
  other arithmetic  3.25 us (2%)
    all_gather x1, waiting for transfers between devices, local(): full_cot = lax.all_gather(cotangent, 'row', axis=0, tiled=True)  61.1 us
    all_gather x1, waiting for transfers between devices, local(): full_inputs = lax.all_gather(inputs, 'col', axis=0, tiled=True)  22.5 us
    all_gather x1, blocking collectives, gathered_total(): return lax.all_gather(value, axis).sum(0)  18.8 us
    reduce_scatter x1, waiting for transfers between devices, local(): lax.psum_scatter(back_part, 'col', scatter_dimension=0, tiled=True)  15.8 us
    dot_general x1, matrix products, local(): lax.dot_general(scaled_in, scaled_cot, (((0,), (0,)), ((), ())), preferre...  12.9 us
    dot_general x2, matrix products, member_sums(): return jnp.dot(one_hot.T, values, precision=highest)  9.29 us
    dot_general x1, matrix products, local(): pre_part = jnp.dot(scaled_in, weight, preferred_element_type=jnp.float32)  7.7 us
    all_to_all x1, starting transfers between devices, from_everyone(): return lax.all_to_all(copies, axis, split_axis=0, concat_axis=0, tiled=True)  7.28 us
  transfers between devices with their start and end apart: 4, of which 3 were waited for; matrix products, arithmetic and copies ran while one was open for 26% of the time, Pallas kernels for 0%

commit v1 on v0

--- a/solution.py
+++ b/solution.py
@@ -28,7 +28,9 @@
     one_hot = (member[:, None] == jnp.arange(n_members, dtype=jnp.int32)[None, :]).astype(
         jnp.float32
     )
-    full_inputs = lax.all_gather(inputs, "col", axis=0, tiled=True)
+    full_inputs = jnp.concatenate(
+        lax.all_to_all(jnp.stack([inputs] * lax.axis_size("col")), "col", 0, 0), axis=0
+    )
     full_cot = lax.all_gather(cotangent, "row", axis=0, tiled=True)
     r_rows = jnp.dot(one_hot, scale_in, precision=highest)
     s_rows = jnp.dot(one_hot, scale_out, precision=highest)

time: 196 us -> 279 us (1.42)
  waiting for transfers between devices: 101 us -> 177 us
  starting transfers between devices: 7.39 us -> 12.4 us
  matrix products: 48.2 us -> 44.8 us
    all_to_all x0 -> x1, waiting for transfers between devices: none -> 114 us  [local(): lax.all_to_all(jnp.stack([inputs] * lax.axis_size('col')), 'col', 0, 0)]
    all_gather x1 -> x0, waiting for transfers between devices: 22.5 us -> none  [local(): full_inputs = lax.all_gather(inputs, 'col', axis=0, tiled=True)]
    reduce_scatter x1, waiting for transfers between devices: 15.8 us -> 0.01 us  [local(): lax.psum_scatter(back_part, 'col', scatter_dimension=0, tiled=True)]
    all_to_all x0 -> x1, starting transfers between devices: none -> 7.32 us  [local(): lax.all_to_all(jnp.stack([inputs] * lax.axis_size('col')), 'col', 0, 0)]
    dot_general x1, matrix products: 7.7 us -> 4.53 us  [local(): pre_part = jnp.dot(scaled_in, weight, preferred_element_type=jnp.float32)]
  transfers between devices with their start and end apart: 4 -> 4, of which waited for: 3 -> 2; matrix products, arithmetic and copies ran while one was open for 26% -> 13% of each run, Pallas kernels for 0% -> 0%
where the time goes in v1:
time: 279 us; the launch traced here: 277 us
  waiting for transfers between devices  177 us (63%)
  matrix products  44.8 us (16%)
  blocking collectives  19.4 us (7%)
  between operations  14.1 us (5%)
  starting transfers between devices  12.4 us (4%)
  local copies, waits for them, and re-layouts  6.32 us (2%)
  other arithmetic  3.25 us (1%)
    all_to_all x1, waiting for transfers between devices, local(): lax.all_to_all(jnp.stack([inputs] * lax.axis_size('col')), 'col', 0, 0)  114 us
    all_gather x1, waiting for transfers between devices, local(): full_cot = lax.all_gather(cotangent, 'row', axis=0, tiled=True)  61.9 us
    all_gather x1, blocking collectives, gathered_total(): return lax.all_gather(value, axis).sum(0)  19.4 us
    dot_general x1, matrix products, local(): lax.dot_general(scaled_in, scaled_cot, (((0,), (0,)), ((), ())), preferre...  10.2 us
    dot_general x2, matrix products, member_sums(): return jnp.dot(one_hot.T, values, precision=highest)  9.83 us
    dot_general x1, matrix products, local(): r_rows = jnp.dot(one_hot, scale_in, precision=highest)  7.54 us
    all_to_all x1, starting transfers between devices, local(): lax.all_to_all(jnp.stack([inputs] * lax.axis_size('col')), 'col', 0, 0)  7.32 us
    dot_general x1, matrix products, local(): lax.dot_general(scaled_cot, weight, (((1,), (1,)), ((), ())), preferred_e...  7.12 us
  transfers between devices with their start and end apart: 4, of which 2 were waited for; matrix products, arithmetic and copies ran while one was open for 13% of the time, Pallas kernels for 0%

profile of v1, /device:TPU:2, one launch (start us, length us, event | category | flops | bytes accessed | tf_op | source)
XLA Modules:
  0.0 277.3 jit_solution(3898294739384454740)
XLA Ops:
  7.2 0.0 copy-start
  7.2 0.0 all-gather.3.cloned.1.call-start
  7.2 0.7 all-gather.3.cloned.1.call-update
  7.9 0.0 reduce-scatter.2.cloned.1.call-start
  8.0 61.9 %all-gather.3.cloned.1.call-done = bf16[2048,1024]{1,0:T(8,128)(2,1)} async-done(((bf16[128,1024]{1,0:T(8,128)(2,1)}), bf16[2048,1024]{1,0:T(8,128)(2,1)}) %all-gather.3.cloned.1.call-update) | async-done | bytes 4194320 | tf_op jit(solution)/shard_map/all_gather | solution.py:34
  69.8 5.6 %fusion = bf16[2048,1024]{1,0:T(8,128)(2,1)S(1)} fusion(bf16[2048,1024]{1,0:T(8,128)(2,1)} %all-gather.3.cloned.1.call-done, f32[8,1024]{1,0:T(8,128)} %param.10, s32[2048]{0:T(1024)} %param.11), kind=kOutput, calls=%fused_computation.4 | convolution fusion | flops 207634432 | bytes 8429568 | tf_op jit(solution)/shard_map/dot_general | solution.py:36
  75.4 0.0 copy-start.2
  75.4 1.9 copy-done.2
  77.4 0.0 copy-done
  77.4 7.1 %fusion.9 = f32[2048,1024]{1,0:T(8,128)} fusion(bf16[2048,1024]{1,0:T(8,128)(2,1)S(1)} %fusion, bf16[1024,1024]{1,0:T(8,128)(2,1)S(1)} %copy-done), kind=kOutput, calls=%fused_computation.16 | convolution fusion | flops 4294967296 | bytes 14680064 | tf_op jit(solution)/shard_map/dot_general | solution.py:45
  84.5 0.0 copy-start.5
  84.5 0.0 reduce-scatter.2.cloned.1.call-update
  84.5 0.9 copy-done.5
  85.4 2.5 stack.2
  88.0 0.0 copy-start.4
  88.0 0.0 copy-start.6
  88.0 7.3 %all-to-all-start = ((bf16[16,128,1024]{2,1,0:T(8,128)(2,1)}), bf16[16,128,1024]{2,1,0:T(8,128)(2,1)}, u32[]{:S(2)}, u32[]{:S(2)}) async-start(bf16[16,128,1024]{2,1,0:T(8,128)(2,1)} %stack.2), calls=%async_computation.1 | async-start | bytes 8388608 | tf_op jit(solution)/shard_map/all_to_all | solution.py:32
  95.3 114.5 %all-to-all-done = bf16[16,128,1024]{2,1,0:T(8,128)(2,1)} async-done(((bf16[16,128,1024]{2,1,0:T(8,128)(2,1)}), bf16[16,128,1024]{2,1,0:T(8,128)(2,1)}, u32[]{:S(2)}, u32[]{:S(2)}) %all-to-all-start) | async-done | bytes 4194336 | tf_op jit(solution)/shard_map/all_to_all | solution.py:32
  209.8 0.0 copy-done.4
  209.8 0.0 copy-done.6
  209.8 7.5 %fusion.2 = (bf16[2048,1024]{1,0:T(8,128)(2,1)S(1)}, f32[2048,1024]{1,0:T(8,128)}) fusion(bf16[16,128,1024]{2,1,0:T(8,128)(2,1)} %all-to-all-done, f32[8,1024]{1,0:T(8,128)S(1)} %copy-done.6, s32[2048]{0:T(1024)S(1)} %copy-done.4), kind=kOutput, calls=%fused_computation.6 | convolution fusion | flops 207634432 | bytes 16818176 | tf_op jit(solution)/shard_map/dot_general | solution.py:35
  217.3 0.0 copy-start.3
  217.3 0.0 copy-start.1
  217.3 4.5 %fusion.11 = f32[2048,1024]{1,0:T(8,128)S(1)} fusion(bf16[2048,1024]{1,0:T(8,128)(2,1)S(1)} %get-tuple-element.4, bf16[1024,1024]{1,0:T(8,128)(2,1)S(1)} %copy-done), kind=kOutput, calls=%fused_computation.18 | convolution fusion | flops 4294967296 | bytes 14680064 | tf_op jit(solution)/shard_map/dot_general | solution.py:40
  221.9 0.0 copy-done.3
  221.9 0.0 copy-done.1
  221.9 3.4 %fusion.1 = f32[8,1024]{1,0:T(8,128)S(1)} fusion(f32[2048,1024]{1,0:T(8,128)S(1)} %fusion.11, bf16[2048,1024]{1,0:T(8,128)(2,1)S(1)} %copy-done.1, s32[2048]{0:T(1024)S(1)} %copy-done.4), kind=kOutput, calls=%fused_computation.5 | convolution fusion | flops 205537280 | bytes 12623872 | tf_op jit(solution)/shard_map/dot_general | solution.py:23
  225.3 0.9 broadcast_in_dim.2
  226.2 5.0 %all-to-all-start.1 = ((f32[16,8,1024]{2,1,0:T(8,128)}), f32[16,8,1024]{2,1,0:T(8,128)S(1)}, u32[]{:S(2)}, u32[]{:S(2)}) async-start(f32[16,8,1024]{2,1,0:T(8,128)} %broadcast_in_dim.2), calls=%async_computation.2 | async-start | bytes 1048576 | tf_op jit(solution)/shard_map/all_to_all | solution.py:11
  231.2 10.2 %fusion.10 = f32[1024,1024]{1,0:T(8,128)} fusion(bf16[2048,1024]{1,0:T(8,128)(2,1)} %copy-done.3, bf16[2048,1024]{1,0:T(8,128)(2,1)} %copy-done.2), kind=kOutput, calls=%fused_computation.17 | convolution fusion | flops 4294967296 | bytes 12582912 | tf_op jit(solution)/shard_map/dot_general | solution.py:53
  241.4 6.4 %fusion.3 = f32[8,1024]{1,0:T(8,128)S(1)} fusion(f32[2048,1024]{1,0:T(8,128)} %fusion.9, bf16[2048,1024]{1,0:T(8,128)(2,1)} %bitcast.1, s32[2048]{0:T(1024)S(1)} %copy-done.4), kind=kOutput, calls=%fused_computation.7 | convolution fusion | flops 205537280 | bytes 12623872 | tf_op jit(solution)/shard_map/dot_general | solution.py:23
  247.8 19.4 %all-gather = f32[128,1024]{1,0:T(8,128)S(1)} all-gather(f32[8,1024]{1,0:T(8,128)S(1)} %fusion.3), channel_id=2, replica_groups=mesh['row'=16,'col'=16] {'col'}, dimensions={0}, use_global_device_ids=true | all-gather | bytes 557056 | tf_op jit(solution)/shard_map/all_gather | solution.py:19
  267.2 0.6 bitcast_reduce_fusion
  267.8 0.0 all-to-all-done.1
  267.8 0.6 reduce_sum.19
  268.5 0.0 reduce-scatter.2.cloned.1.call-done
  268.5 2.0 multiply_convert_fusion
Async XLA Ops:
  7.2 70.2 %copy-start = (bf16[1024,1024]{1,0:T(8,128)(2,1)S(1)}, bf16[1024,1024]{1,0:T(8,128)(2,1)}, u32[]{:S(2)}) copy-start(bf16[1024,1024]{1,0:T(8,128)(2,1)} %param.7) | copy-start | bytes 6291460
  7.2 62.6 %all-gather.3.cloned.1.call-start = ((), (), s32[]{:S(2)}) async-start(), calls=%async_computation.3 | async-start | bytes 4456448 | tf_op jit(solution)/shard_map/all_gather | solution.py:34
  7.9 260.6 %reduce-scatter.2.cloned.1.call-start = ((), (), s32[]{:S(2)}) async-start(), calls=%async_computation.4 | async-start | bytes 8912896 | tf_op jit(solution)/shard_map/reduce_scatter | solution.py:50
  75.4 1.9 copy-start.2
  84.5 0.9 copy-start.5
  88.0 121.8 %copy-start.4 = (s32[2048]{0:T(1024)S(1)}, s32[2048]{0:T(1024)}, u32[]{:S(2)}) copy-start(s32[2048]{0:T(1024)} %param.11) | copy-start | bytes 24580
  88.0 121.8 %copy-start.6 = (f32[8,1024]{1,0:T(8,128)S(1)}, f32[8,1024]{1,0:T(8,128)}, u32[]{:S(2)}) copy-start(f32[8,1024]{1,0:T(8,128)} %param.9) | copy-start | bytes 98308
  88.0 121.8 %all-to-all-start = ((bf16[16,128,1024]{2,1,0:T(8,128)(2,1)}), bf16[16,128,1024]{2,1,0:T(8,128)(2,1)}, u32[]{:S(2)}, u32[]{:S(2)}) async-start(bf16[16,128,1024]{2,1,0:T(8,128)(2,1)} %stack.2), calls=%async_computation.1 | async-start | bytes 8388608 | tf_op jit(solution)/shard_map/all_to_all | solution.py:32
  217.3 4.5 %copy-start.3 = (bf16[2048,1024]{1,0:T(8,128)(2,1)}, bf16[2048,1024]{1,0:T(8,128)(2,1)S(1)}, u32[]{:S(2)}) copy-start(bf16[2048,1024]{1,0:T(8,128)(2,1)S(1)} %get-tuple-element.4) | copy-start | bytes 12582916
  217.3 4.5 %copy-start.1 = (bf16[2048,1024]{1,0:T(8,128)(2,1)S(1)}, bf16[2048,1024]{1,0:T(8,128)(2,1)}, u32[]{:S(2)}) copy-start(bf16[2048,1024]{1,0:T(8,128)(2,1)} %all-gather.3.cloned.1.call-done) | copy-start | bytes 12582916
  226.2 41.6 %all-to-all-start.1 = ((f32[16,8,1024]{2,1,0:T(8,128)}), f32[16,8,1024]{2,1,0:T(8,128)S(1)}, u32[]{:S(2)}, u32[]{:S(2)}) async-start(f32[16,8,1024]{2,1,0:T(8,128)} %broadcast_in_dim.2), calls=%async_computation.2 | async-start | bytes 1048576 | tf_op jit(solution)/shard_map/all_to_all | solution.py:11
Sparse Core Ops, SparseCore 0:
  10.4 59.3 all-gather.2
  84.6 155.0 reduce-scatter.1
